TPU v7x, 32 devices: a whole 2x2x4 slice. The times are simulated.
32 devices in a mesh: hst: 4 (over y, core), dev: 8 (over z, x).
Axes of the slice: x: 2, y: 2, z: 4, core: 2. Of those that a mesh axis runs over, the one named last changes fastest.
Arguments:
- hot_rows: bfloat16 [4096, 768], replicated, may hold values from -6 to 6
- cold_rows: bfloat16 [32768, 768], P(('hst', 'dev')), may hold values from -6 to 6
- hot_mask: int32 [65536], P(('hst', 'dev')), may hold values from 0 to 1, as said below
- hot_id: int32 [65536], P(('hst', 'dev')), may hold values from 0 to 4095
- cold_owner: int32 [65536], P(('hst', 'dev')), may hold values from 0 to 31, as said below
- cold_pos: int32 [65536], P(('hst', 'dev')), may hold values from 0 to 63, as said below
- cold_send: int32 [32, 2048], P(('hst', 'dev')), may hold values from 0 to 1023
- adjacency_one: int32 [65536, 15], P(('hst', 'dev')), may hold values from 0 to 2047
- adjacency_two: int32 [16384, 15], P(('hst', 'dev')), may hold values from 0 to 2303
- halo_send: int32 [32, 256], P(('hst', 'dev')), may hold values from 0 to 2047
- self_first: bfloat16 [768, 1024], replicated, may hold values from -0.21875 to 0.21875
- neigh_first: bfloat16 [768, 1024], replicated, may hold values from -0.21875 to 0.21875
- bn_gain: float32 [1024], replicated, may hold values from 0.1 to 1.9
- bn_shift: float32 [1024], replicated, may hold values from -3 to 3
- self_second: bfloat16 [1024, 153], replicated, may hold values from -0.1875 to 0.1875
- neigh_second: bfloat16 [1024, 153], replicated, may hold values from -0.1875 to 0.1875
Outputs:
- logits: float32 [16384, 153], P(('hst', 'dev'))
Inputs may be any that keep to these rules, and one draw needn't show every extreme that they name: Each device has exactly 1536 nodes with hot_mask 0. `cold_owner`: for each device and owner, at most 64 of the device's nodes with hot_mask 0 name that owner; some owner is named by exactly 64 of them on every device. `cold_pos`: the nodes of one device with hot_mask 0 and the same owner have distinct slots.
All inputs are finite; a program needn't handle non-finite values.
Results may differ from a plain program's by a relative error of at most 0.003.
The roundings to bfloat16 on the way count: a program that leaves them out, or rounds other values in their place, can miss the bound.
Values may be sent and summed in bfloat16 or wider, within the bound.
A program may use at most 128 MiB of HBM per device.

v0:
```python
import functools

import jax
import jax.numpy as jnp
from jax import lax
from jax.experimental import pallas as pl
from jax.experimental.pallas import tpu as pltpu
from jax.sharding import PartitionSpec as P

epsilon = 1e-05
LANES = 128
MIB = 1024 * 1024


def whole(shape):
    return pl.BlockSpec(shape, lambda *_: (0,) * len(shape))


def block_of(rows, wanted):
    while rows % wanted:
        wanted //= 2
    return wanted


def one_hot(index, width):
    columns = lax.broadcasted_iota(jnp.int32, (index.shape[0], width), 1)
    return jnp.where(index == columns, 1.0, 0.0).astype(jnp.bfloat16)


def select_kernel(index_ref, rows_ref, out_ref):
    picks = one_hot(index_ref[...], rows_ref.shape[0])
    out_ref[...] = jnp.dot(picks, rows_ref[...], preferred_element_type=jnp.float32).astype(out_ref.dtype)


def select_rows(rows, index):
    count, width = index.shape[0], rows.shape[1]
    step = block_of(count, 512)
    return pl.pallas_call(
        select_kernel,
        grid=(count // step,),
        in_specs=[pl.BlockSpec((step, 1), lambda i: (i, 0)), whole(rows.shape)],
        out_specs=pl.BlockSpec((step, width), lambda i: (i, 0)),
        out_shape=jax.ShapeDtypeStruct((count, width), rows.dtype),
        compiler_params=pltpu.CompilerParams(vmem_limit_bytes=16 * MIB),
        name="select_rows",
    )(index[:, None], rows)


def count_kernel(index_ref, out_ref):
    rows, fanout = index_ref.shape
    width = out_ref.shape[1]
    part = 16

    def some_rows(step, carry):
        here = pl.ds(pl.multiple_of(step * part, part), part)
        index = index_ref[here, :]
        lane = lax.broadcasted_iota(jnp.int32, (part, LANES), 1).astype(jnp.int16)
        spread = [
            jnp.broadcast_to(index[:, k : k + 1], (part, LANES)).astype(jnp.int16) for k in range(fanout)
        ]
        one, none = jnp.ones((part, LANES), jnp.bfloat16), jnp.zeros((part, LANES), jnp.bfloat16)
        for tile in range(width // LANES):
            columns = lane + jnp.int16(tile * LANES)
            total = none
            for k in range(fanout):
                total = total + jnp.where(spread[k] == columns, one, none)
            out_ref[here, tile * LANES : (tile + 1) * LANES] = total
        return carry

    lax.fori_loop(0, rows // part, some_rows, 0)


def count_matrix(index, width):
    rows, fanout = index.shape
    step = block_of(rows, 512)
    return pl.pallas_call(
        count_kernel,
        grid=(rows // step,),
        in_specs=[pl.BlockSpec((step, fanout), lambda i: (i, 0))],
        out_specs=pl.BlockSpec((step, width), lambda i: (i, 0)),
        out_shape=jax.ShapeDtypeStruct((rows, width), jnp.bfloat16),
        compiler_params=pltpu.CompilerParams(vmem_limit_bytes=16 * MIB),
        cost_estimate=pl.CostEstimate(
            flops=rows * width * fanout * 100, bytes_accessed=rows * width * 2, transcendentals=0
        ),
        name="count_matrix",
    )(index)


def first_kernel(blocks, fanout, arrived_ref, place_ref, hot_ref, counts_ref, self_ref, neigh_ref,
                 pre_ref, stats_ref, features):
    step = pl.program_id(0)
    rows = place_ref.shape[0]

    @pl.when(step < blocks)
    def _():
        place = one_hot(place_ref[...], arrived_ref.shape[0])
        cold = jnp.dot(place, arrived_ref[...], preferred_element_type=jnp.float32)
        here = pl.ds(pl.multiple_of(step * rows, rows), rows)
        features[here, :] = cold.astype(jnp.bfloat16) + hot_ref[...]

    @pl.when(step >= blocks)
    def _():
        here = pl.ds(pl.multiple_of((step - blocks) * rows, rows), rows)
        total = jnp.dot(counts_ref[...], features[...], preferred_element_type=jnp.float32)
        mean = (total / fanout).astype(jnp.bfloat16)
        pre = jnp.dot(features[here, :], self_ref[...], preferred_element_type=jnp.float32)
        pre = pre + jnp.dot(mean, neigh_ref[...], preferred_element_type=jnp.float32)
        pre_ref[...] = pre
        both = jnp.concatenate(
            [jnp.sum(pre, axis=0, keepdims=True), jnp.sum(pre * pre, axis=0, keepdims=True)], axis=0
        )

        @pl.when(step == blocks)
        def _():
            stats_ref[...] = both

        @pl.when(step > blocks)
        def _():
            stats_ref[...] += both


def first_layer(arrived, place, hot_feat, counts, self_first, neigh_first, fanout):
    nodes, width = hot_feat.shape
    units = self_first.shape[1]
    step = block_of(nodes, 512)
    blocks = nodes // step
    early = lambda i: (jnp.minimum(i, blocks - 1), 0)
    late = lambda i: (jnp.maximum(i - blocks, 0), 0)
    return pl.pallas_call(
        functools.partial(first_kernel, blocks, fanout),
        grid=(2 * blocks,),
        in_specs=[
            whole(arrived.shape),
            pl.BlockSpec((step, place.shape[1]), early),
            pl.BlockSpec((step, width), early),
            pl.BlockSpec((step, counts.shape[1]), late),
            whole(self_first.shape),
            whole(neigh_first.shape),
        ],
        out_specs=[pl.BlockSpec((step, units), late), whole((2, units))],
        out_shape=[
            jax.ShapeDtypeStruct((nodes, units), jnp.float32),
            jax.ShapeDtypeStruct((2, units), jnp.float32),
        ],
        scratch_shapes=[pltpu.VMEM((nodes, width), jnp.bfloat16)],
        compiler_params=pltpu.CompilerParams(vmem_limit_bytes=36 * MIB),
        name="first_layer",
    )(arrived, place, hot_feat, counts, self_first, neigh_first)


def stats_kernel(hosts, within, own_ref, out_ref, near, far, part, send_near, recv_near, send_far, recv_far):
    host, lane = lax.axis_index("hst"), lax.axis_index("dev")
    barrier = pltpu.get_barrier_semaphore()
    for away in range(1, within):
        pl.semaphore_signal(barrier, inc=1, device_id={"dev": lax.rem(lane + away, within)},
                            device_id_type=pl.DeviceIdType.MESH)
    for away in range(1, hosts):
        pl.semaphore_signal(barrier, inc=1, device_id={"hst": lax.rem(host + away, hosts)},
                            device_id_type=pl.DeviceIdType.MESH)
    pl.semaphore_wait(barrier, within + hosts - 2)

    def exchange(source, slots, axis, me, size, send, recv):
        copies = []
        for away in range(1, size):
            copy = pltpu.make_async_remote_copy(
                src_ref=source, dst_ref=slots.at[away - 1], send_sem=send.at[away - 1],
                recv_sem=recv.at[away - 1], device_id={axis: lax.rem(me + away, size)},
                device_id_type=pl.DeviceIdType.MESH,
            )
            copy.start()
            copies.append(copy)
        for copy in copies:
            copy.wait()
        total = source[...]
        for away in range(1, size):
            total = total + slots[away - 1]
        return total

    part[...] = exchange(own_ref, near, "dev", lane, within, send_near, recv_near)
    out_ref[...] = exchange(part, far, "hst", host, hosts, send_far, recv_far)


def sum_stats(own, hosts, within):
    return pl.pallas_call(
        functools.partial(stats_kernel, hosts, within),
        in_specs=[pl.BlockSpec(memory_space=pltpu.VMEM)],
        out_specs=pl.BlockSpec(memory_space=pltpu.VMEM),
        out_shape=jax.ShapeDtypeStruct(own.shape, own.dtype),
        scratch_shapes=[
            pltpu.VMEM((within - 1,) + own.shape, own.dtype),
            pltpu.VMEM((hosts - 1,) + own.shape, own.dtype),
            pltpu.VMEM(own.shape, own.dtype),
            pltpu.SemaphoreType.DMA((within - 1,)),
            pltpu.SemaphoreType.DMA((within - 1,)),
            pltpu.SemaphoreType.DMA((hosts - 1,)),
            pltpu.SemaphoreType.DMA((hosts - 1,)),
        ],
        compiler_params=pltpu.CompilerParams(
            collective_id=0, has_side_effects=True, vmem_limit_bytes=4 * MIB
        ),
        name="sum_stats",
    )(own)


def norm_kernel(total_rows, pre_ref, stats_ref, gain_ref, shift_ref, picks_ref, hidden_ref, boundary_ref, held):
    step = pl.program_id(0)
    mean = stats_ref[0:1, :] / total_rows
    variance = stats_ref[1:2, :] / total_rows - mean * mean
    scale = lax.rsqrt(variance + epsilon)
    hidden = jnp.maximum((pre_ref[...] - mean) * scale * gain_ref[...] + shift_ref[...], 0.0)
    hidden = hidden.astype(jnp.bfloat16)
    hidden_ref[...] = hidden
    picks = one_hot(picks_ref[...] - step * hidden.shape[0], hidden.shape[0])
    picked = jnp.dot(picks, hidden, preferred_element_type=jnp.float32)

    @pl.when(step == 0)
    def _():
        held[...] = picked

    @pl.when(step > 0)
    def _():
        held[...] += picked

    @pl.when(step == pl.num_programs(0) - 1)
    def _():
        boundary_ref[...] = held[...].astype(jnp.bfloat16)


def norm_layer(pre, stats, gain, shift, picks, total_rows):
    nodes, units = pre.shape
    step = block_of(nodes, 512)
    edge = picks.shape[0]
    return pl.pallas_call(
        functools.partial(norm_kernel, total_rows),
        grid=(nodes // step,),
        in_specs=[
            pl.BlockSpec((step, units), lambda i: (i, 0)),
            whole(stats.shape),
            whole((1, units)),
            whole((1, units)),
            whole((edge, 1)),
        ],
        out_specs=[pl.BlockSpec((step, units), lambda i: (i, 0)), whole((edge, units))],
        out_shape=[
            jax.ShapeDtypeStruct((nodes, units), jnp.bfloat16),
            jax.ShapeDtypeStruct((edge, units), jnp.bfloat16),
        ],
        scratch_shapes=[pltpu.VMEM((edge, units), jnp.float32)],
        compiler_params=pltpu.CompilerParams(vmem_limit_bytes=20 * MIB),
        name="norm_layer",
    )(pre, stats, gain[None, :], shift[None, :], picks)


def last_kernel(within, fanout, boundary_ref, hidden_ref, counts_ref, self_ref, neigh_ref, out_ref,
                received, send, recv, own_sem):
    lane = lax.axis_index("dev")
    nodes = hidden_ref.shape[0]
    targets = counts_ref.shape[0]
    slots = boundary_ref.shape[0] // within
    barrier = pltpu.get_barrier_semaphore()
    for away in range(1, within):
        pl.semaphore_signal(barrier, inc=1, device_id={"dev": lax.rem(lane + away, within)},
                            device_id_type=pl.DeviceIdType.MESH)
    pl.semaphore_wait(barrier, within - 1)
    mine = pl.ds(pl.multiple_of(lane * slots, slots), slots)
    copies = []
    for away in range(1, within):
        peer = lax.rem(lane + away, within)
        copy = pltpu.make_async_remote_copy(
            src_ref=boundary_ref.at[pl.ds(pl.multiple_of(peer * slots, slots), slots)],
            dst_ref=received.at[mine],
            send_sem=send.at[away - 1], recv_sem=recv.at[away - 1], device_id={"dev": peer},
            device_id_type=pl.DeviceIdType.MESH,
        )
        copy.start()
        copies.append(copy)
    own = pltpu.make_async_copy(boundary_ref.at[mine], received.at[mine], own_sem)
    own.start()
    total = jnp.dot(counts_ref[:, :nodes], hidden_ref[...], preferred_element_type=jnp.float32)
    scores = jnp.dot(hidden_ref[:targets, :], self_ref[...], preferred_element_type=jnp.float32)
    own.wait()
    for copy in copies:
        copy.wait()
    total = total + jnp.dot(counts_ref[:, nodes:], received[...], preferred_element_type=jnp.float32)
    mean = (total / fanout).astype(jnp.bfloat16)
    out_ref[...] = scores + jnp.dot(mean, neigh_ref[...], preferred_element_type=jnp.float32)


def last_layer(boundary, hidden, counts, self_second, neigh_second, within, fanout):
    return pl.pallas_call(
        functools.partial(last_kernel, within, fanout),
        in_specs=[pl.BlockSpec(memory_space=pltpu.VMEM)] * 5,
        out_specs=pl.BlockSpec(memory_space=pltpu.VMEM),
        out_shape=jax.ShapeDtypeStruct((counts.shape[0], self_second.shape[1]), jnp.float32),
        scratch_shapes=[
            pltpu.VMEM(boundary.shape, boundary.dtype),
            pltpu.SemaphoreType.DMA((within - 1,)),
            pltpu.SemaphoreType.DMA((within - 1,)),
            pltpu.SemaphoreType.DMA,
        ],
        compiler_params=pltpu.CompilerParams(
            collective_id=1, has_side_effects=True, vmem_limit_bytes=24 * MIB
        ),
        name="last_layer",
    )(boundary, hidden, counts, self_second, neigh_second)


def local(
    hot_rows,
    cold_rows,
    hot_mask,
    hot_id,
    cold_owner,
    cold_pos,
    cold_send,
    adjacency_one,
    adjacency_two,
    halo_send,
    self_first,
    neigh_first,
    bn_gain,
    bn_shift,
    self_second,
    neigh_second,
):
    hosts = lax.axis_size("hst")
    within = lax.axis_size("dev")
    nodes = hot_mask.shape[0]
    outgoing = select_rows(cold_rows, cold_send[0])
    slots = outgoing.shape[0] // (hosts * within)
    arrived = lax.all_to_all(outgoing, ("hst", "dev"), split_axis=0, concat_axis=0, tiled=True)

    hot_feat = jnp.where(
        hot_mask[:, None] == 1, hot_rows.at[hot_id].get(mode="promise_in_bounds"), 0
    )
    source = jnp.where(hot_mask == 1, -1, cold_owner * slots + cold_pos)
    place = source[:, None]
    counts_one = count_matrix(adjacency_one, nodes)
    counts_two = count_matrix(adjacency_two, nodes + halo_send.shape[1])
    picks = halo_send[0][:, None]

    pre, own = first_layer(
        arrived, place, hot_feat, counts_one, self_first, neigh_first, adjacency_one.shape[1]
    )
    stats = sum_stats(own, hosts, within)
    hidden, boundary = norm_layer(pre, stats, bn_gain, bn_shift, picks, nodes * hosts * within)
    return last_layer(
        boundary, hidden, counts_two, self_second, neigh_second, within, adjacency_two.shape[1]
    )


def solution(mesh):
    placed = (
        P(),
        P(("hst", "dev"), None),
        P(("hst", "dev")),
        P(("hst", "dev")),
        P(("hst", "dev")),
        P(("hst", "dev")),
        P(("hst", "dev"), None),
        P(("hst", "dev"), None),
        P(("hst", "dev"), None),
        P(("hst", "dev"), None),
        P(),
        P(),
        P(),
        P(),
        P(),
        P(),
    )
    return jax.shard_map(
        local, mesh=mesh, in_specs=placed, out_specs=P(("hst", "dev"), None), check_vma=False
    )
```

profile of v0, /device:TPU:0, one launch (start us, length us, event | category | flops | bytes accessed | tf_op | source)
XLA Modules:
  0.0 157.1 jit_solution(126388632367002551)
XLA Ops:
  0.0 1.1 copy.22.index_ref
  1.1 0.0 copy-start.11
  1.1 1.4 copy-done.11
  2.5 4.5 %select_rows.1 = bf16[2048,768]{1,0:T(8,128)(2,1)S(1)} custom-call(s32[2048,1]{1,0:T(8,128)S(1)} %copy.22.index_ref, bf16[1024,768]{1,0:T(8,128)(2,1)S(1)} %copy-done.11), custom_call_target="tpu_custom_call" | custom-call | tf_op jit(solution)/shard_map/select_rows/pallas_call | solution.py:38
  7.0 0.0 copy-start.1
  7.0 1.7 %copy-done.1 = bf16[2048,768]{1,0:T(8,128)(2,1)} copy-done((bf16[2048,768]{1,0:T(8,128)(2,1)}, bf16[2048,768]{1,0:T(8,128)(2,1)S(1)}, u32[]{:S(2)}) %copy-start.1) | copy-done | bytes 3145752
  8.7 0.0 copy-start.17
  8.7 0.0 copy-start.18
  8.7 0.0 copy-start.19
  8.7 0.0 copy-start.16
  8.7 0.0 copy-start.20
  8.7 7.3 %all-to-all-start = ((bf16[32,64,768]{2,1,0:T(8,128)(2,1)}), bf16[32,64,768]{2,1,0:T(8,128)(2,1)S(1)}, u32[]{:S(2)}, u32[]{:S(2)}) async-start(bf16[32,64,768]{2,1,0:T(8,128)(2,1)} %bitcast.8), calls=%async_computation | async-start | bytes 6291456 | tf_op jit(solution)/shard_map/all_to_all | solution.py:332
  16.0 0.0 copy-done.17
  16.0 0.0 copy-done.18
  16.1 0.0 copy-done.19
  16.1 1.4 copy.24.place_ref
  17.5 0.0 copy-done.16
  17.5 1.3 copy.23.index_ref
  18.8 0.0 copy-done.20
  18.8 0.1 copy.25.picks_ref
  18.9 0.9 copy.26.index_ref
  19.8 2.0 %copy.27.self_ref = bf16[1024,153]{1,0:T(8,128)(2,1)} copy(bf16[1024,153]{0,1:T(8,128)(2,1)} %param.30) | data formatting | bytes 626688 | tf_op args[14]
  21.8 2.0 %copy.28.neigh_ref = bf16[1024,153]{1,0:T(8,128)(2,1)} copy(bf16[1024,153]{0,1:T(8,128)(2,1)} %param.31) | data formatting | bytes 626688 | tf_op args[15]
  23.8 0.7 fusion
  24.5 13.7 %gather_fusion = bf16[2048,768]{1,0:T(8,128)(2,1)} fusion(bf16[4096,768]{1,0:T(8,128)(2,1)} %param.16, s32[2048]{0:T(1024)S(1)} %fusion), kind=kCustom, calls=%fused_computation | custom fusion | bytes 6299648 | tf_op jit(solution)/shard_map/gather | solution.py:335
  38.2 0.0 copy-start.12
  38.2 6.0 %count_matrix.3.counts_ref = bf16[512,2304]{1,0:T(8,128)(2,1)S(1)} custom-call(s32[512,15]{1,0:T(8,128)S(1)} %copy.26.index_ref), custom_call_target="tpu_custom_call" | custom-call | flops 1769472000 | bytes 2359296 | tf_op jit(solution)/shard_map/count_matrix/pallas_call | solution.py:76
  44.2 0.0 copy-start.5
  44.2 1.4 copy-done.5
  45.6 0.0 copy-done.12
  45.6 0.0 copy-start.15
  45.6 22.4 %count_matrix.2.counts_ref = bf16[2048,2048]{1,0:T(8,128)(2,1)S(1)} custom-call(s32[2048,15]{1,0:T(8,128)S(1)} %copy-done.12), custom_call_target="tpu_custom_call" | custom-call | flops 6291456000 | bytes 8388608 | tf_op jit(solution)/shard_map/count_matrix/pallas_call | solution.py:76
  68.0 0.0 copy-start.2
  68.0 3.3 %copy-done.2 = bf16[2048,2048]{1,0:T(8,128)(2,1)} copy-done((bf16[2048,2048]{1,0:T(8,128)(2,1)}, bf16[2048,2048]{1,0:T(8,128)(2,1)S(1)}, u32[]{:S(2)}) %copy-start.2) | copy-done | bytes 8388632
  71.3 0.0 copy-done.15
  71.3 1.9 %broadcast_select_fusion.hot_ref = bf16[2048,768]{1,0:T(8,128)(2,1)} fusion(bf16[2048,768]{1,0:T(8,128)(2,1)S(1)} %copy-done.15, pred[2048]{0:T(1024)(128)(4,1)S(1)} %get-tuple-element.14), kind=kLoop, calls=%fused_computation.1 | loop fusion | flops 1572864 | bytes 6293504 | tf_op jit(solution)/shard_map/jit(_where)/select_n | solution.py:334
  73.2 15.4 %all-to-all-done = bf16[32,64,768]{2,1,0:T(8,128)(2,1)S(1)} async-done(((bf16[32,64,768]{2,1,0:T(8,128)(2,1)}), bf16[32,64,768]{2,1,0:T(8,128)(2,1)S(1)}, u32[]{:S(2)}, u32[]{:S(2)}) %all-to-all-start) | async-done | bytes 3145760 | tf_op jit(solution)/shard_map/all_to_all | solution.py:332
  88.6 0.0 copy-start
  88.6 1.9 %copy-done = bf16[2048,768]{1,0:T(8,128)(2,1)S(1)} copy-done((bf16[2048,768]{1,0:T(8,128)(2,1)S(1)}, bf16[2048,768]{1,0:T(8,128)(2,1)}, u32[]{:S(2)}) %copy-start) | copy-done | bytes 3145752
  90.5 0.0 copy-start.4
  90.5 1.2 copy-done.4
  91.7 0.0 copy-start.9
  91.7 1.4 copy-done.9
  93.1 0.0 copy-start.10
  93.1 1.4 copy-done.10
  94.5 0.0 copy-start.13
  94.5 0.0 copy-start.14
  94.5 29.6 %first_layer.1 = (f32[2048,1024]{1,0:T(8,128)}, f32[2,1024]{1,0:T(2,128)S(1)}) custom-call(bf16[2048,768]{1,0:T(8,128)(2,1)S(1)} %bitcast.7, s32[2048,1]{1,0:T(8,128)S(1)} %copy-done.4, bf16[2048,768]{1,0:T(8,128)(2,1)S(1)} %copy-done, bf16[2048,2048]{1,0:T(8,128)(2,1)} %copy-done.2, bf16[768,1024]{1,0:T(8,128)(2,1)S(1)} %copy-done.9, ...), custom_call_target="tpu_custom_call" | custom-call | tf_op jit(solution)/shard_map/first_layer/pallas_call | solution.py:130
  124.1 8.7 %sum_stats.1.stats_ref = f32[2,1024]{1,0:T(2,128)S(1)} custom-call(f32[2,1024]{1,0:T(2,128)S(1)} %get-tuple-element.10.own_ref), custom_call_target="tpu_custom_call" | custom-call | tf_op jit(solution)/shard_map/sum_stats/pallas_call | solution.py:185
  132.8 0.0 copy-done.13
  132.8 0.0 copy-done.14
  132.8 0.0 copy-start.3
  132.8 3.4 %copy-done.3 = f32[2048,1024]{1,0:T(8,128)S(1)} copy-done((f32[2048,1024]{1,0:T(8,128)S(1)}, f32[2048,1024]{1,0:T(8,128)}, u32[]{:S(2)}) %copy-start.3) | copy-done | bytes 8388632
  136.2 0.0 copy-start.6
  136.2 0.0 copy-start.7
  136.2 0.0 copy-start.8
  136.2 3.2 %norm_layer.1 = (bf16[2048,1024]{1,0:T(8,128)(2,1)S(1)}, bf16[256,1024]{1,0:T(8,128)(2,1)S(1)}) custom-call(f32[2048,1024]{1,0:T(8,128)S(1)} %copy-done.3, f32[2,1024]{1,0:T(2,128)S(1)} %sum_stats.1.stats_ref, f32[1,1024]{1,0:T(1,128)S(1)} %bitcast.9, f32[1,1024]{1,0:T(1,128)S(1)} %bitcast.10, s32[256,1]{1,0:T(8,128)S(1)} %copy.25.picks_ref), custom_call_target="tpu_custom_call" | custom-call | tf_op jit(solution)/shard_map/norm_layer/pallas_call | solution.py:234
  139.5 0.0 copy-done.6
  139.5 0.0 copy-done.7
  139.5 0.0 copy-done.8
  139.5 16.7 %last_layer.1 = f32[512,153]{1,0:T(8,128)S(1)} custom-call(bf16[256,1024]{1,0:T(8,128)(2,1)S(1)} %get-tuple-element.11.boundary_ref, bf16[2048,1024]{1,0:T(8,128)(2,1)S(1)} %get-tuple-element.12.hidden_ref, bf16[512,2304]{1,0:T(8,128)(2,1)S(1)} %copy-done.6, bf16[1024,153]{1,0:T(8,128)(2,1)S(1)} %copy-done.7, bf16[1024,153]{1,0:T(8,128)(2,1)S(1)} %copy-done.8), custom_call_target="tpu_custom_call" | custom-call | tf_op jit(solution)/shard_map/last_layer/pallas_call | solution.py:291
  156.2 0.9 copy.29
  (1 shorter events, 0.0 us)
Async XLA Ops:
  1.1 1.4 copy-start.11
  7.0 1.7 %copy-start.1 = (bf16[2048,768]{1,0:T(8,128)(2,1)}, bf16[2048,768]{1,0:T(8,128)(2,1)S(1)}, u32[]{:S(2)}) copy-start(bf16[2048,768]{1,0:T(8,128)(2,1)S(1)} %select_rows.1) | copy-start | bytes 9437188
  8.7 7.4 %copy-start.17 = (s32[2048]{0:T(1024)S(1)}, s32[2048]{0:T(1024)}, u32[]{:S(2)}) copy-start(s32[2048]{0:T(1024)} %param.21) | copy-start | bytes 24580
  8.7 7.4 %copy-start.18 = (s32[2048]{0:T(1024)S(1)}, s32[2048]{0:T(1024)}, u32[]{:S(2)}) copy-start(s32[2048]{0:T(1024)} %param.20) | copy-start | bytes 24580
  8.7 7.4 %copy-start.19 = (s32[2048]{0:T(1024)S(1)}, s32[2048]{0:T(1024)}, u32[]{:S(2)}) copy-start(s32[2048]{0:T(1024)} %param.18) | copy-start | bytes 24580
  8.7 8.8 %copy-start.16 = (s32[2048,15]{0,1:T(8,128)S(1)}, s32[2048,15]{0,1:T(8,128)}, u32[]{:S(2)}) copy-start(s32[2048,15]{0,1:T(8,128)} %param.23) | copy-start | bytes 368644
  8.7 10.1 %copy-start.20 = (s32[1,256]{1,0:T(1,128)S(1)}, s32[1,256]{1,0:T(1,128)}, u32[]{:S(2)}) copy-start(s32[1,256]{1,0:T(1,128)} %param.25) | copy-start | bytes 3076
  8.7 79.9 %all-to-all-start = ((bf16[32,64,768]{2,1,0:T(8,128)(2,1)}), bf16[32,64,768]{2,1,0:T(8,128)(2,1)S(1)}, u32[]{:S(2)}, u32[]{:S(2)}) async-start(bf16[32,64,768]{2,1,0:T(8,128)(2,1)} %bitcast.8), calls=%async_computation | async-start | bytes 6291456 | tf_op jit(solution)/shard_map/all_to_all | solution.py:332
  38.2 7.4 %copy-start.12 = (s32[2048,15]{1,0:T(8,128)S(1)}, s32[2048,15]{1,0:T(8,128)}, u32[]{:S(2)}) copy-start(s32[2048,15]{1,0:T(8,128)} %copy.23.index_ref) | copy-start | bytes 368644
  44.2 1.4 copy-start.5
  45.6 25.7 %copy-start.15 = (bf16[2048,768]{1,0:T(8,128)(2,1)S(1)}, bf16[2048,768]{1,0:T(8,128)(2,1)}, u32[]{:S(2)}) copy-start(bf16[2048,768]{1,0:T(8,128)(2,1)} %gather_fusion) | copy-start | bytes 9437188
  68.0 3.3 %copy-start.2 = (bf16[2048,2048]{1,0:T(8,128)(2,1)}, bf16[2048,2048]{1,0:T(8,128)(2,1)S(1)}, u32[]{:S(2)}) copy-start(bf16[2048,2048]{1,0:T(8,128)(2,1)S(1)} %count_matrix.2.counts_ref) | copy-start | bytes 25165828
  88.6 1.9 %copy-start = (bf16[2048,768]{1,0:T(8,128)(2,1)S(1)}, bf16[2048,768]{1,0:T(8,128)(2,1)}, u32[]{:S(2)}) copy-start(bf16[2048,768]{1,0:T(8,128)(2,1)} %broadcast_select_fusion.hot_ref) | copy-start | bytes 9437188
  90.5 1.2 copy-start.4
  91.7 1.4 copy-start.9
  93.1 1.4 copy-start.10
  94.5 38.3 %copy-start.13 = (f32[1024]{0:T(1024)S(1)}, f32[1024]{0:T(1024)}, u32[]{:S(2)}) copy-start(f32[1024]{0:T(1024)} %param.28) | copy-start | bytes 12292
  94.5 38.3 %copy-start.14 = (f32[1024]{0:T(1024)S(1)}, f32[1024]{0:T(1024)}, u32[]{:S(2)}) copy-start(f32[1024]{0:T(1024)} %param.29) | copy-start | bytes 12292
  132.8 3.4 %copy-start.3 = (f32[2048,1024]{1,0:T(8,128)S(1)}, f32[2048,1024]{1,0:T(8,128)}, u32[]{:S(2)}) copy-start(f32[2048,1024]{1,0:T(8,128)} %get-tuple-element.9.pre_ref) | copy-start | bytes 25165828
  136.2 3.3 %copy-start.6 = (bf16[512,2304]{1,0:T(8,128)(2,1)S(1)}, bf16[512,2304]{1,0:T(8,128)(2,1)}, u32[]{:S(2)}) copy-start(bf16[512,2304]{1,0:T(8,128)(2,1)} %copy-done.5) | copy-start | bytes 7077892
  136.2 3.3 %copy-start.7 = (bf16[1024,153]{1,0:T(8,128)(2,1)S(1)}, bf16[1024,153]{1,0:T(8,128)(2,1)}, u32[]{:S(2)}) copy-start(bf16[1024,153]{1,0:T(8,128)(2,1)} %copy.27.self_ref) | copy-start | bytes 940036
  136.2 3.3 %copy-start.8 = (bf16[1024,153]{1,0:T(8,128)(2,1)S(1)}, bf16[1024,153]{1,0:T(8,128)(2,1)}, u32[]{:S(2)}) copy-start(bf16[1024,153]{1,0:T(8,128)(2,1)} %copy.28.neigh_ref) | copy-start | bytes 940036
where the time goes:
time: 158 us; the launch traced here: 157 us
  Pallas kernels  91 us (58%)
  local copies, waits for them, and re-layouts  40.5 us (26%)
  waiting for transfers between devices  15.4 us (10%)
  starting transfers between devices  7.33 us (5%)
  other arithmetic  2.64 us (2%)
    pallas_call x1, Pallas kernels, first_layer(): pl.pallas_call(functools.partial(first_kernel, blocks, fanout), grid=(2 *...  29.6 us
    pallas_call x2, Pallas kernels, count_matrix(): pl.pallas_call(count_kernel, grid=(rows // step,), in_specs=[pl.BlockSpec...  28.4 us
    unnamed x46, local copies, waits for them, and re-layouts  23.3 us
    pallas_call x1, Pallas kernels, last_layer(): pl.pallas_call(functools.partial(last_kernel, within, fanout), in_specs=[...  16.7 us
    all_to_all x1, waiting for transfers between devices, local(): lax.all_to_all(outgoing, ('hst', 'dev'), split_axis=0, concat_axis=0, til...  15.4 us
    gather x1, local copies, waits for them, and re-layouts, local(): hot_rows.at[hot_id].get(mode='promise_in_bounds')  13.7 us
    pallas_call x1, Pallas kernels, sum_stats(): pl.pallas_call(functools.partial(stats_kernel, hosts, within), in_specs=[...  8.71 us
    all_to_all x1, starting transfers between devices, local(): lax.all_to_all(outgoing, ('hst', 'dev'), split_axis=0, concat_axis=0, til...  7.33 us
  transfers between devices with their start and end apart: 1, of which 1 were waited for; matrix products, arithmetic and copies ran while one was open for 15% of the time, Pallas kernels for 18%

commit v1 on v0

v1 whole, which is shorter than its diff:
```python
import functools

import jax
import jax.numpy as jnp
from jax import lax
from jax.experimental import pallas as pl
from jax.experimental.pallas import tpu as pltpu
from jax.sharding import PartitionSpec as P

epsilon = 1e-05
LANES = 128
MIB = 1024 * 1024
MESH = pl.DeviceIdType.MESH
BF16, F32, I32 = jnp.bfloat16, jnp.float32, jnp.int32


def dot(a, b):
    return jnp.dot(a, b, preferred_element_type=F32)


def dot_nt(a, b):
    return lax.dot_general(a, b, (((1,), (1,)), ((), ())), preferred_element_type=F32)


def hot_where(match, value=1.0):
    return jnp.where(match, value, 0.0).astype(BF16)


def iota(shape, axis):
    return lax.broadcasted_iota(I32, shape, axis)


def spread(column):
    return jnp.broadcast_to(column, (column.shape[0], LANES))


def one_hot_tiles(wide, tiles):
    lane = iota(wide.shape, 1)
    return jnp.concatenate([hot_where(wide == lane + LANES * t) for t in range(tiles)], axis=1)


def look_up(table, index):
    low, high = index & (LANES - 1), index >> 7
    out = jnp.zeros_like(index)
    for t in range(table.shape[0]):
        row = jnp.broadcast_to(table[t : t + 1, :], index.shape)
        out = jnp.where(high == t, jnp.take_along_axis(row, low, axis=1, mode="promise_in_bounds"), out)
    return out


def running_count(flags):
    tiles = flags.shape[0]
    marks = flags.astype(BF16)
    before = hot_where(iota((LANES, LANES), 0) < iota((LANES, LANES), 1))
    within = dot(marks, before)
    totals = dot(marks, jnp.ones((LANES, LANES), BF16)).astype(BF16)
    above = hot_where(iota((tiles, tiles), 1) < iota((tiles, tiles), 0))
    return (within + dot(above, totals)).astype(I32)


def digits_of(slots, valid, words):
    low, high = slots & (LANES - 1), slots >> 7
    parts = [low.astype(F32)]
    for word in range(words):
        here = valid & ((high >> 3) == word)
        parts.append(jnp.where(here, (jnp.int32(1) << ((high & 7) * 4)), 0).astype(F32))
    return jnp.concatenate(parts, axis=0).astype(BF16)


def count_block(digits_ref, start, rows, fanout, lines, words, tiles, put):
    digits = digits_ref[pl.ds(start, rows), :]
    lane = iota((rows, LANES), 1)
    sums = [jnp.zeros((rows, LANES), I32) for _ in range(words)]
    for k in range(fanout):
        match = spread(digits[:, k : k + 1]) == lane
        for word in range(words):
            at = (word + 1) * lines + k
            sums[word] = sums[word] + jnp.where(match, spread(digits[:, at : at + 1]), 0)
    for t in range(tiles):
        put(t, ((sums[t // 8] >> (4 * (t % 8))) & 15).astype(F32).astype(BF16))


def program(dims, hot_hbm, cold_hbm, mask_ref, hot_id_ref, owner_ref, pos_ref, send_ref, near_ref, next_ref,
            halo_ref, self_hbm, neigh_hbm, gain_ref, shift_ref, self2_ref, neigh2_ref, out_ref,
            cold, outgoing, arrived, hot, extra, counts, edge_counts, total, edge_total, pre, last_counts,
            self_w, neigh_w, edge_out, edge_in, wide, used, digits, slots_near, slots_next, rows, tables, square,
            chunk_rows, stat_own, stat_near, stat_part, stat_far,
            load, send, recv, send_edge, recv_edge, edge_copy, send_near, recv_near, send_far, recv_far):
    hosts, within, fanout, fanout2, total_rows = dims
    devices = hosts * within
    slots, width = outgoing.shape
    units = pre.shape[1]
    cap = slots // devices
    half = within // 2
    tiles = slots // LANES
    chunk, chunks = counts.shape[2], counts.shape[0]
    edge = edge_out.shape[0]
    share = edge // within
    targets = out_ref.shape[1]
    host, lane = lax.axis_index("hst"), lax.axis_index("dev")
    me = host * within + lane
    side = lane // half

    def at(peer):
        return {"hst": peer // within, "dev": lax.rem(peer, within)}

    loads = [
        pltpu.make_async_copy(source, target, load.at[i])
        for i, (source, target) in enumerate(
            [(cold_hbm, cold), (hot_hbm, hot), (self_hbm, self_w), (neigh_hbm, neigh_w)]
        )
    ]
    loads[0].start()

    barrier = pltpu.get_barrier_semaphore()

    def greet(away, carry):
        pl.semaphore_signal(barrier, inc=1, device_id=at(lax.rem(me + away, devices)), device_id_type=MESH)
        return carry

    lax.fori_loop(1, devices, greet, 0)

    square[...] = jnp.zeros_like(square)
    for t in range(tiles):
        square[t : t + 1, :] = send_ref[:, t * LANES : (t + 1) * LANES].astype(F32)
    turned = square[...].T.astype(I32)
    for t in range(tiles):
        wide[t * LANES : (t + 1) * LANES, :] = spread(turned[:, t : t + 1])
    loads[0].wait()

    def pick(step, carry):
        here = pl.ds(pl.multiple_of(step * 256, 256), 256)
        outgoing[here, :] = dot(one_hot_tiles(wide[here, :], cold.shape[0] // LANES), cold[...]).astype(BF16)
        return carry

    lax.fori_loop(0, slots // 256, pick, 0)
    pl.semaphore_wait(barrier, devices - 1)

    def block(peer):
        return pl.ds(pl.multiple_of(peer * cap, cap), cap)

    def row_copy(peer):
        away = lax.rem(peer - me + devices, devices)
        return pltpu.make_async_remote_copy(
            src_ref=outgoing.at[block(peer)], dst_ref=arrived.at[block(me)],
            send_sem=send.at[away], recv_sem=recv.at[away], device_id=at(peer), device_id_type=MESH,
        )

    def peer_of(step, flip, towards):
        h = lax.rem(host + (step // half) * towards + hosts, hosts)
        return h * within + lax.rem(side + flip, 2) * half + lax.rem(lane + step, half)

    def start_far(step, carry):
        row_copy(peer_of(step, 1, 1)).start()
        return carry

    def start_near(step, carry):
        row_copy(peer_of(step, 0, 1)).start()
        return carry

    lax.fori_loop(0, hosts * half, start_far, 0)
    lax.fori_loop(1, hosts * half, start_near, 0)
    for copy in loads[1:]:
        copy.start()
    arrived[block(me), :] = outgoing[block(me), :]

    def to_table(row, i):
        for t in range(tiles):
            tables[i, t : t + 1, :] = row[:, t * LANES : (t + 1) * LANES]

    def to_row(table, i):
        for t in range(tiles):
            rows[i : i + 1, t * LANES : (t + 1) * LANES] = table[t : t + 1, :]

    cold_node = mask_ref[...] != 1
    key = jnp.where(cold_node, owner_ref[...] * cap + pos_ref[...], -1)
    to_table(key, 0)
    key_table = tables[0]
    high = hot_where((key >> 7) == iota((tiles, slots), 0))
    low = hot_where((key & (LANES - 1)) == iota((LANES, slots), 0))
    taken = dot_nt(high, low) > 0.5
    free_rank = running_count(jnp.where(taken, 0.0, 1.0))
    to_row(jnp.where(taken, -1, free_rank), 0)
    rank = rows[0:1, :]
    slot = iota((1, slots), 1)
    high = (rank >> 7) == iota((tiles, slots), 0)
    low = hot_where((rank & (LANES - 1)) == iota((LANES, slots), 0))
    free_slot = dot_nt(hot_where(high, (slot >> 7).astype(F32)), low).astype(I32) * LANES
    free_slot = free_slot + dot_nt(hot_where(high, (slot & (LANES - 1)).astype(F32)), low).astype(I32)
    hot_rank = running_count(jnp.where(key_table < 0, 1.0, 0.0))
    tables[1] = jnp.where(key_table < 0, look_up(free_slot, hot_rank), key_table)
    to_row(tables[1], 1)

    slots_near[...] = jnp.zeros_like(slots_near)
    slots_near[0:fanout, :] = near_ref[...]
    slots_next[...] = jnp.zeros_like(slots_next)
    slots_next[0:fanout2, :] = next_ref[...]
    lines, lines2 = slots_near.shape[0], slots_next.shape[0]

    def map_near(step, carry):
        here = pl.ds(pl.multiple_of(step * LANES, LANES), LANES)
        slots_near[:, here] = look_up(tables[1], slots_near[:, here])
        return carry

    lax.fori_loop(0, slots // LANES, map_near, 0)

    def map_next(step, carry):
        here = pl.ds(pl.multiple_of(step * LANES, LANES), LANES)
        index = slots_next[:, here]
        slots_next[:, here] = jnp.where(index < slots, look_up(tables[1], index), index)
        return carry

    lax.fori_loop(0, targets // LANES, map_next, 0)
    words, words2 = -(-tiles // 8), -(-(tiles + edge // LANES) // 8)
    near_digits = digits_of(slots_near[...], iota((lines, slots), 0) < fanout, words)
    own = jnp.where(cold_node, 0, hot_id_ref[...])
    own_lines = jnp.concatenate(
        [
            jnp.broadcast_to((own >> 7).astype(F32), (lines, slots)),
            jnp.broadcast_to((own & (LANES - 1)).astype(F32), (lines, slots)),
            jnp.broadcast_to(jnp.where(cold_node, 0.0, 1.0), (lines, slots)),
        ],
        axis=0,
    ).astype(BF16)
    near_digits = jnp.concatenate([near_digits, own_lines], axis=0)
    node_slot = rows[1:2, :]
    first_own = (words + 1) * lines

    for copy in loads[1:]:
        copy.wait()

    def build(step, carry):
        start = pl.multiple_of(step * 256, 256)
        here = pl.ds(start, 256)
        mine = hot_where(node_slot == iota((256, slots), 0) + start)
        found = dot_nt(mine, near_digits).astype(I32)
        digits[:, 0 : found.shape[1]] = found
        is_hot = found[:, first_own + 2 * lines : first_own + 2 * lines + 1] > 0
        row = found[:, first_own : first_own + 1] * LANES + found[:, first_own + lines : first_own + lines + 1]
        row = spread(jnp.where(is_hot, row, -1))
        used[here, :] = row
        for part in range(4):
            size = hot.shape[0] // 4
            picks = one_hot_tiles(row - part * size, size // LANES)
            product = dot(picks, hot[part * size : (part + 1) * size, :])
            got = product if part == 0 else got + product
        extra[here, :] = got.astype(BF16)

        def some(part, carry):
            at_row = pl.multiple_of(part * 32, 32)

            def put(t, value):
                counts[t * LANES // chunk, pl.ds(start + at_row, 32),
                       t * LANES % chunk : t * LANES % chunk + LANES] = value

            count_block(digits, at_row, 32, fanout, lines, words, tiles, put)
            return carry

        lax.fori_loop(0, 256 // 32, some, 0)
        return carry

    lax.fori_loop(0, slots // 256, build, 0)

    for t in range(edge // LANES):
        index = jnp.broadcast_to(halo_ref[:, t * LANES : (t + 1) * LANES], (8, LANES))
        index = look_up(tables[1], index)
        pair = jnp.concatenate([(index >> 7).astype(F32), (index & (LANES - 1)).astype(F32)], axis=0).astype(BF16)
        eye = hot_where(iota((LANES, LANES), 0) == iota((LANES, LANES), 1))
        found = dot_nt(eye, pair).astype(I32)
        column = spread(found[:, 0:1] * LANES + found[:, 8:9])
        picks = one_hot_tiles(column, tiles)
        for c in range(chunks):
            edge_counts[c, t * LANES : (t + 1) * LANES, :] = dot(picks, counts[c]).astype(BF16)
            edge_counts[c, edge + t * LANES : edge + (t + 1) * LANES, :] = picks[:, c * chunk : (c + 1) * chunk]

    for t in range(targets // LANES):
        there = slice(t * LANES, (t + 1) * LANES)
        index = slots_next[:, there]
        parts = digits_of(index, iota((lines2, LANES), 0) < fanout2, words2)
        index = jnp.broadcast_to(tables[1, t : t + 1, :], (16, LANES))
        pair = jnp.concatenate([(index >> 7).astype(F32), (index & (LANES - 1)).astype(F32)], axis=0).astype(BF16)
        parts = jnp.concatenate([parts, pair], axis=0)
        eye = hot_where(iota((LANES, LANES), 0) == iota((LANES, LANES), 1))
        found = dot_nt(eye, parts).astype(I32)
        digits[0:LANES, 0 : found.shape[1]] = found
        at_own = (words2 + 1) * lines2
        column = spread(found[:, at_own : at_own + 1] * LANES + found[:, at_own + 16 : at_own + 17])
        last_counts[targets + t * LANES : targets + (t + 1) * LANES, 0:slots] = one_hot_tiles(column, tiles)

        def some(part, carry):
            at_row = pl.multiple_of(part * 32, 32)

            def put(tile, value):
                last_counts[pl.ds(t * LANES + at_row, 32), tile * LANES : (tile + 1) * LANES] = value

            count_block(digits, at_row, 32, fanout2, lines2, words2, tiles + edge // LANES, put)
            return carry

        lax.fori_loop(0, LANES // 32, some, 0)

    total[...] = jnp.zeros_like(total)
    edge_total[...] = jnp.zeros_like(edge_total)

    def arrive(step, carry):
        h = lax.rem(host - lax.rem(step, hosts) + hosts, hosts)
        which = h * 2 + lax.rem(side + step // hosts, 2)

        def await_one(q, carry):
            peer = which * half + q

            @pl.when(peer != me)
            def _():
                away = lax.rem(me - peer + devices, devices)
                pltpu.make_async_remote_copy(
                    src_ref=outgoing.at[block(me)], dst_ref=arrived.at[block(peer)],
                    send_sem=send.at[away], recv_sem=recv.at[away], device_id=at(peer), device_id_type=MESH,
                ).wait_recv()

            return carry

        lax.fori_loop(0, half, await_one, 0)
        here = pl.ds(pl.multiple_of(which * chunk, chunk), chunk)
        mine = jnp.concatenate([used[here, :]] * (width // LANES), axis=1) < 0
        chunk_rows[...] = jnp.where(mine, arrived[here, :].astype(F32), extra[here, :].astype(F32)).astype(BF16)
        pre[here, :] = dot(chunk_rows[...], self_w[...])
        edge_total[...] += dot(edge_counts[which], chunk_rows[...])

        def gather(part, carry):
            there = pl.ds(pl.multiple_of(part * 512, 512), 512)
            total[there, :] += dot(counts[which, there, :], chunk_rows[...])
            return carry

        lax.fori_loop(0, slots // 512, gather, 0)
        return carry

    lax.fori_loop(0, chunks, arrive, 0)

    edge_mean = (edge_total[0:edge, :] * (1.0 / fanout)).astype(BF16)
    edge_pre = dot(edge_total[edge : 2 * edge, :].astype(BF16), self_w[...]) + dot(edge_mean, neigh_w[...])
    centre = jnp.mean(edge_pre, axis=0, keepdims=True)
    edge_out[...] = (edge_pre - centre).astype(BF16)

    def part_of(peer):
        return pl.ds(pl.multiple_of(peer * share, share), share)

    edge_copies = []
    for away in range(1, within):
        peer = lax.rem(lane + away, within)
        edge_copies.append(pltpu.make_async_remote_copy(
            src_ref=edge_out.at[part_of(peer)], dst_ref=edge_in.at[part_of(lane)],
            send_sem=send_edge.at[away - 1], recv_sem=recv_edge.at[away - 1],
            device_id={"dev": peer}, device_id_type=MESH,
        ))
        edge_copies[-1].start()
    edge_in[part_of(lane), :] = edge_out[part_of(lane), :]

    def finish(step, sums):
        here = pl.ds(pl.multiple_of(step * 256, 256), 256)
        mean = (total[here, :] * (1.0 / fanout)).astype(BF16)
        value = pre[here, :] + dot(mean, neigh_w[...])
        pre[here, :] = value
        return sums[0] + jnp.sum(value, axis=0, keepdims=True), sums[1] + jnp.sum(value * value, axis=0, keepdims=True)

    zero = jnp.zeros((1, units), F32)
    first, second = lax.fori_loop(0, slots // 256, finish, (zero, zero))
    stat_own[...] = jnp.concatenate([first, second, centre, zero], axis=0)

    def exchange(source, landing, axis, index, size, send_sem, recv_sem):
        copies = []
        for away in range(1, size):
            copies.append(pltpu.make_async_remote_copy(
                src_ref=source, dst_ref=landing.at[away - 1], send_sem=send_sem.at[away - 1],
                recv_sem=recv_sem.at[away - 1], device_id={axis: lax.rem(index + away, size)},
                device_id_type=MESH,
            ))
            copies[-1].start()
        for copy in copies:
            copy.wait()
        value = source[...]
        for away in range(1, size):
            value = value + landing[away - 1]
        return value

    stat_part[...] = exchange(stat_own, stat_near, "dev", lane, within, send_near, recv_near)
    sums = exchange(stat_part, stat_far, "hst", host, hosts, send_far, recv_far)
    mean = sums[0:1, :] / total_rows
    variance = sums[1:2, :] / total_rows - mean * mean
    scale = lax.rsqrt(variance + epsilon) * gain_ref[...]
    shift = shift_ref[...]

    def normal(step, carry):
        here = pl.ds(pl.multiple_of(step * 256, 256), 256)
        hidden = jnp.maximum((pre[here, :] - mean) * scale + shift, 0.0).astype(BF16)
        for c in range(units // chunk):
            counts[c, here, :] = hidden[:, c * chunk : (c + 1) * chunk]
        return carry

    lax.fori_loop(0, slots // 256, normal, 0)
    for copy in edge_copies:
        copy.wait()
    for away in range(within):
        there = part_of(lax.rem(lane - away + within, within))
        origin = centre if away == 0 else stat_near[away - 1][2:3, :]
        value = edge_in[there, :].astype(F32) + (origin - mean)
        edge_in[there, :] = jnp.maximum(value * scale + shift, 0.0).astype(BF16)
    out_ref[...] = jnp.zeros_like(out_ref)

    def second_layer(c, carry):
        there = pl.ds(pl.multiple_of(c * chunk, chunk), chunk)
        both = dot(last_counts[:, 0:slots], counts[c])
        near = both[0:targets, :] + dot(last_counts[0:targets, slots:], edge_in[:, there])
        near = (near * (1.0 / fanout2)).astype(BF16)
        out_ref[...] += dot_nt(neigh2_ref[:, there], near) + dot_nt(self2_ref[:, there], both[targets:, :].astype(BF16))
        return carry

    lax.fori_loop(0, units // chunk, second_layer, 0)

    def drain(away, carry):
        row_copy(lax.rem(me + away, devices)).wait_send()
        return carry

    lax.fori_loop(1, devices, drain, 0)


def local(hot_rows, cold_rows, hot_mask, hot_id, cold_owner, cold_pos, cold_send, adjacency_one, adjacency_two,
          halo_send, self_first, neigh_first, bn_gain, bn_shift, self_second, neigh_second):
    hosts, within = lax.axis_size("hst"), lax.axis_size("dev")
    devices = hosts * within
    nodes, fanout = adjacency_one.shape
    targets, fanout2 = adjacency_two.shape
    slots, edge = cold_send.shape[1], halo_send.shape[1]
    width, units = self_first.shape
    classes = self_second.shape[1]
    assert slots == nodes
    chunk = slots // devices * (within // 2)
    chunks = slots // chunk
    lines, lines2 = -(-fanout // 16) * 16, -(-fanout2 // 16) * 16
    tiles = slots // LANES
    any_space, vmem = pl.BlockSpec(memory_space=pl.ANY), pl.BlockSpec(memory_space=pltpu.VMEM)
    dma = pltpu.SemaphoreType.DMA
    out = pl.pallas_call(
        functools.partial(program, (hosts, within, fanout, fanout2, nodes * devices)),
        in_specs=[any_space] * 2 + [vmem] * 8 + [any_space] * 2 + [vmem] * 4,
        out_specs=vmem,
        out_shape=jax.ShapeDtypeStruct((classes, targets), F32),
        scratch_shapes=[
            pltpu.VMEM(cold_rows.shape, BF16),
            pltpu.VMEM((slots, width), BF16),
            pltpu.VMEM((slots, width), BF16),
            pltpu.VMEM(hot_rows.shape, BF16),
            pltpu.VMEM((slots, width), BF16),
            pltpu.VMEM((chunks, slots, chunk), BF16),
            pltpu.VMEM((chunks, 2 * edge, chunk), BF16),
            pltpu.VMEM((slots, width), F32),
            pltpu.VMEM((2 * edge, width), F32),
            pltpu.VMEM((slots, units), F32),
            pltpu.VMEM((2 * targets, slots + edge), BF16),
            pltpu.VMEM((width, units), BF16),
            pltpu.VMEM((width, units), BF16),
            pltpu.VMEM((edge, units), BF16),
            pltpu.VMEM((edge, units), BF16),
            pltpu.VMEM((slots, LANES), I32),
            pltpu.VMEM((slots, LANES), I32),
            pltpu.VMEM((256, LANES), I32),
            pltpu.VMEM((lines, slots), I32),
            pltpu.VMEM((lines2, targets), I32),
            pltpu.VMEM((8, slots), I32),
            pltpu.VMEM((2, tiles, LANES), I32),
            pltpu.VMEM((LANES, LANES), F32),
            pltpu.VMEM((chunk, width), BF16),
            pltpu.VMEM((4, units), F32),
            pltpu.VMEM((within - 1, 4, units), F32),
            pltpu.VMEM((4, units), F32),
            pltpu.VMEM((hosts - 1, 4, units), F32),
            dma((4,)),
            dma((devices,)),
            dma((devices,)),
            dma((within - 1,)),
            dma((within - 1,)),
            dma,
            dma((within - 1,)),
            dma((within - 1,)),
            dma((hosts - 1,)),
            dma((hosts - 1,)),
        ],
        compiler_params=pltpu.CompilerParams(
            collective_id=0, has_side_effects=True, vmem_limit_bytes=63 * MIB
        ),
        name="sage",
    )(
        hot_rows, cold_rows, hot_mask[None, :], hot_id[None, :], cold_owner[None, :], cold_pos[None, :], cold_send,
        adjacency_one.T, adjacency_two.T, halo_send, self_first, neigh_first, bn_gain[None, :], bn_shift[None, :],
        self_second.T, neigh_second.T,
    )
    return out.T


def solution(mesh):
    owned, split, copied = P(("hst", "dev"), None), P(("hst", "dev")), P()
    placed = (copied, owned) + (split,) * 4 + (owned,) * 4 + (copied,) * 6
    return jax.shard_map(local, mesh=mesh, in_specs=placed, out_specs=owned, check_vma=False)
```

time: 158 us -> 124 us (0.78)
  local copies, waits for them, and re-layouts: 40.5 us -> 1.72 us
  Pallas kernels: 91 us -> 122 us
  waiting for transfers between devices: 15.4 us -> 0 us
  starting transfers between devices: 7.33 us -> 0 us
  other arithmetic: 2.64 us -> 0 us
    pallas_call x7 -> x1, Pallas kernels: 91 us -> 122 us  [local(): pl.pallas_call(functools.partial(program, (hosts, within, fanout, fanout2...]
    unnamed x46 -> x1, local copies, waits for them, and re-layouts: 23.3 us -> 1.72 us
    all_to_all x1 -> x0, waiting for transfers between devices: 15.4 us -> none  [local(): lax.all_to_all(outgoing, ('hst', 'dev'), split_axis=0, concat_axis=0, til...]
    gather x1 -> x0, local copies, waits for them, and re-layouts: 13.7 us -> none  [local(): hot_rows.at[hot_id].get(mode='promise_in_bounds')]
    all_to_all x1 -> x0, starting transfers between devices: 7.33 us -> none  [local(): lax.all_to_all(outgoing, ('hst', 'dev'), split_axis=0, concat_axis=0, til...]
    select_n x2 -> x0, other arithmetic: 1.94 us -> none  [the longest x1 1.94 us: local(): jnp.where(hot_mask[:, None] == 1, hot_rows.at[hot_id].get(mode='promise_i...]
  transfers between devices with their start and end apart: 1 -> 0, of which waited for: 1 -> 0; matrix products, arithmetic and copies ran while one was open for 15% -> 0% of each run, Pallas kernels for 18% -> 0%
where the time goes in v1:
time: 124 us
  Pallas kernels  122 us (98%)
  local copies, waits for them, and re-layouts  1.72 us (1%)
    pallas_call x1, Pallas kernels, local(): pl.pallas_call(functools.partial(program, (hosts, within, fanout, fanout2...  122 us

profile of v1, /device:TPU:0, one launch (start us, length us, event | category | flops | bytes accessed | tf_op | source)
XLA Modules:
  0.0 124.1 jit_solution(5102667198892267548)
XLA Ops:
  0.0 122.4 %sage.1 = f32[153,512]{1,0:T(8,128)} custom-call(bf16[4096,768]{1,0:T(8,128)(2,1)} %hot_hbm.1, bf16[1024,768]{1,0:T(8,128)(2,1)} %cold_hbm.1, s32[1,2048]{1,0:T(1,128)} %bitcast.16, s32[1,2048]{1,0:T(1,128)} %bitcast.17, s32[1,2048]{1,0:T(1,128)} %bitcast.18, s32[1,2048]{1,0:T(1,128)} %bitcast.19, s32[1,2048]{1,0:T(1,128)} %send_ref.1, s32[15,2048]{1,0:T(8,128)} %bitcast.14, ...), custom_call_target="tpu_custom_call" | custom-call | tf_op jit(solution)/shard_map/sage/pallas_call | solution.py:441
  122.4 1.7 %copy.18 = f32[512,153]{0,1:T(8,128)} copy(f32[512,153]{0,1:T(8,128)} %bitcast.11) | data formatting | bytes 626688

commit v2 on v1

v2 whole, which is shorter than its diff:
```python
import functools
import math

import jax
import jax.numpy as jnp
from jax import lax
from jax.experimental import pallas as pl
from jax.experimental.pallas import tpu as pltpu
from jax.sharding import PartitionSpec as P

epsilon = 1e-05
LANES = 128
MIB = 1024 * 1024
SHARES = 4
MESH = pl.DeviceIdType.MESH
BF16, F32, I32 = jnp.bfloat16, jnp.float32, jnp.int32


def dot(a, b):
    return jnp.dot(a, b, preferred_element_type=F32)


def dot_nt(a, b):
    return lax.dot_general(a, b, (((1,), (1,)), ((), ())), preferred_element_type=F32)


def hot_where(match, value=1.0):
    return jnp.where(match, value, 0.0).astype(BF16)


def iota(shape, axis):
    return lax.broadcasted_iota(I32, shape, axis)


def spread(column):
    return jnp.broadcast_to(column, (column.shape[0], LANES))


def one_hot_tiles(wide, tiles):
    lane = iota(wide.shape, 1)
    return jnp.concatenate([hot_where(wide == lane + LANES * t) for t in range(tiles)], axis=1)


def look_up(table, index):
    low, high = index & (LANES - 1), index >> 7
    out = jnp.zeros_like(index)
    for t in range(table.shape[0]):
        row = jnp.broadcast_to(table[t : t + 1, :], index.shape)
        out = jnp.where(high == t, jnp.take_along_axis(row, low, axis=1, mode="promise_in_bounds"), out)
    return out


def running_count(flags):
    tiles = flags.shape[0]
    marks = flags.astype(BF16)
    before = hot_where(iota((LANES, LANES), 0) < iota((LANES, LANES), 1))
    within = dot(marks, before)
    totals = dot(marks, jnp.ones((LANES, LANES), BF16)).astype(BF16)
    above = hot_where(iota((tiles, tiles), 1) < iota((tiles, tiles), 0))
    return (within + dot(above, totals)).astype(I32)


def turned(row):
    return jnp.broadcast_to(row, (LANES, LANES)).T


def inverse_of(row, tiles, value):
    high = (row >> 7) == iota((tiles, row.shape[1]), 0)
    low = hot_where((row & (LANES - 1)) == iota((LANES, row.shape[1]), 0))
    upper = dot_nt(hot_where(high, (value >> 7).astype(F32)), low).astype(I32)
    lower = dot_nt(hot_where(high, (value & (LANES - 1)).astype(F32)), low).astype(I32)
    return upper * LANES + lower


def count_tile(index, fanout, tiles, lows, nibbles, put):
    words = -(-tiles // 8)
    high = index >> 7
    lows[...] = index & (LANES - 1)
    for word in range(words):
        nibbles[word] = jnp.where((high >> 3) == word, jnp.int32(1) << ((high & 7) * 4), 0)
    part = 32
    sums = [[] for _ in range(words)]
    for start in range(0, LANES, part):
        place = iota((part, LANES), 0) + start
        held = [jnp.zeros((part, LANES), I32) for _ in range(words)]
        for k in range(fanout):
            match = jnp.broadcast_to(lows[k : k + 1, :], (part, LANES)) == place
            for word in range(words):
                more = jnp.broadcast_to(nibbles[word, k : k + 1, :], (part, LANES))
                held[word] = held[word] + jnp.where(match, more, 0)
        for word in range(words):
            sums[word].append(held[word])
    for word in range(words):
        across = jnp.concatenate(sums[word], axis=0).T
        for t in range(word * 8, min(tiles, word * 8 + 8)):
            put(t, ((across >> (4 * (t % 8))) & 15).astype(F32).astype(BF16))


def program(dims, hot_hbm, cold_hbm, mask_hbm, hot_id_hbm, owner_hbm, pos_hbm, send_hbm, near_hbm, next_hbm,
            halo_hbm, self_hbm, neigh_hbm, gain_hbm, shift_hbm, self2_hbm, neigh2_hbm, out_ref,
            mask_ref, hot_id_ref, owner_ref, pos_ref, send_ref, near_ref, next_ref, halo_ref, gain_ref, shift_ref,
            self2_ref, neigh2_ref,
            cold, outgoing, arrived, hot, extra, counts, edge_counts, total, edge_total, pre, last_counts,
            self_w, neigh_w, edge_out, edge_in, wide, slots_near, slots_sorted, slots_next, rows, tables, lows, nibbles,
            chunk_rows, stat_own, stat_near, stat_part, stat_far,
            load, send, recv, send_edge, recv_edge, send_near, recv_near, send_far, recv_far):
    hosts, within, fanout, fanout2, total_rows = dims
    devices = hosts * within
    slots, width = outgoing.shape
    units = pre.shape[1]
    cap = slots // devices
    half = within // 2
    tiles = slots // LANES
    chunk, chunks = counts.shape[2], counts.shape[0]
    edge = edge_out.shape[0]
    share = edge // within
    targets = out_ref.shape[1]
    host, lane = lax.axis_index("hst"), lax.axis_index("dev")
    me = host * within + lane
    side = lane // half

    def at(peer):
        return {"hst": peer // within, "dev": lax.rem(peer, within)}

    loads = [
        pltpu.make_async_copy(source, target, load.at[i])
        for i, (source, target) in enumerate(
            [
                (send_hbm, send_ref), (cold_hbm, cold), (mask_hbm, mask_ref), (hot_id_hbm, hot_id_ref),
                (owner_hbm, owner_ref), (pos_hbm, pos_ref), (near_hbm, near_ref), (next_hbm, next_ref),
                (halo_hbm, halo_ref), (gain_hbm, gain_ref), (shift_hbm, shift_ref), (self2_hbm, self2_ref),
                (neigh2_hbm, neigh2_ref), (hot_hbm, hot), (self_hbm, self_w), (neigh_hbm, neigh_w),
            ]
        )
    ]
    early, middle, late = loads[:2], loads[2:13], loads[13:]
    for copy in early:
        copy.start()

    barrier = pltpu.get_barrier_semaphore()

    def greet(away, carry):
        pl.semaphore_signal(barrier, inc=1, device_id=at(lax.rem(me + away, devices)), device_id_type=MESH)
        return carry

    lax.fori_loop(1, devices, greet, 0)

    def block(peer):
        return pl.ds(pl.multiple_of(peer * cap, cap), cap)

    def row_copy(peer):
        away = lax.rem(peer - me + devices, devices)
        return pltpu.make_async_remote_copy(
            src_ref=outgoing.at[block(peer)], dst_ref=arrived.at[block(me)],
            send_sem=send.at[away], recv_sem=recv.at[away], device_id=at(peer), device_id_type=MESH,
        )

    def chunk_at(step, towards):
        h = lax.rem(host + lax.rem(step, hosts) * towards + hosts, hosts)
        return h * 2 + lax.rem(side + 1 + step // hosts, 2)

    def pick(step):
        begin = chunk_at(step, 1) * chunk
        columns = [
            turned(send_ref[:, pl.ds(pl.multiple_of(begin + t, LANES), LANES)]) for t in range(0, chunk, LANES)
        ]
        picks = one_hot_tiles(jnp.concatenate(columns, axis=0), cold.shape[0] // LANES)
        outgoing[pl.ds(pl.multiple_of(begin, chunk), chunk), :] = dot(picks, cold[...]).astype(BF16)

    def start(step):
        def start_one(q, carry):
            peer = chunk_at(step, 1) * half + lax.rem(lane + q, half)

            @pl.when(peer != me)
            def _():
                row_copy(peer).start()

            return carry

        lax.fori_loop(0, half, start_one, 0)

    def pick_and_start(step, carry):
        pick(step)
        start(step)
        return carry

    for copy in early:
        copy.wait()
    pick(0)
    pl.semaphore_wait(barrier, devices - 1)
    start(0)
    lax.fori_loop(1, chunks, pick_and_start, 0)
    for copy in middle + late:
        copy.start()
    arrived[block(me), :] = outgoing[block(me), :]

    def to_table(row, i):
        for t in range(tiles):
            tables[i, t : t + 1, :] = row[:, t * LANES : (t + 1) * LANES]

    def to_row(table, i):
        for t in range(tiles):
            rows[i : i + 1, t * LANES : (t + 1) * LANES] = table[t : t + 1, :]

    for copy in middle:
        copy.wait()
    cold_node = mask_ref[...] != 1
    key = jnp.where(cold_node, owner_ref[...] * cap + pos_ref[...], -1)
    to_table(key, 0)
    key_table = tables[0]
    high = hot_where((key >> 7) == iota((tiles, slots), 0))
    low = hot_where((key & (LANES - 1)) == iota((LANES, slots), 0))
    taken = dot_nt(high, low) > 0.5
    free_rank = running_count(jnp.where(taken, 0.0, 1.0))
    to_row(jnp.where(taken, -1, free_rank), 0)
    free_slot = inverse_of(rows[0:1, :], tiles, iota((1, slots), 1))
    hot_rank = running_count(jnp.where(key_table < 0, 1.0, 0.0))
    tables[1] = jnp.where(key_table < 0, look_up(free_slot, hot_rank), key_table)
    to_row(tables[1], 1)

    to_row(inverse_of(rows[1:2, :], tiles, iota((1, slots), 1)), 2)

    lines = slots_near.shape[0]
    slots_near[...] = jnp.zeros_like(slots_near)
    slots_near[0:fanout, :] = near_ref[...]
    slots_next[...] = jnp.zeros_like(slots_next)
    slots_next[0:fanout2, :] = next_ref[...]

    def map_near(step, carry):
        here = pl.ds(pl.multiple_of(step * LANES, LANES), LANES)
        slots_near[:, here] = look_up(tables[1], slots_near[:, here])
        return carry

    lax.fori_loop(0, tiles, map_near, 0)
    slots_near[fanout : fanout + 1, :] = jnp.where(cold_node, -1, hot_id_ref[...])

    def sort_near(step, carry):
        here = pl.ds(pl.multiple_of(step * LANES, LANES), LANES)
        node = jnp.broadcast_to(rows[2:3, here], (lines, LANES))
        low, high = node & (LANES - 1), node >> 7
        out = jnp.zeros_like(node)
        for t in range(tiles):
            part = slots_near[:, t * LANES : (t + 1) * LANES]
            out = jnp.where(high == t, jnp.take_along_axis(part, low, axis=1, mode="promise_in_bounds"), out)
        slots_sorted[:, here] = out
        wide[here, :] = turned(out[fanout : fanout + 1, :])
        return carry

    lax.fori_loop(0, tiles, sort_near, 0)

    def map_next(step, carry):
        here = pl.ds(pl.multiple_of(step * LANES, LANES), LANES)
        index = slots_next[:, here]
        slots_next[:, here] = jnp.where(index < slots, look_up(tables[1], index), index)
        return carry

    lax.fori_loop(0, targets // LANES, map_next, 0)
    for copy in late:
        copy.wait()

    def build(step, carry):
        first = pl.multiple_of(step * 256, 256)
        here = pl.ds(first, 256)
        for part in range(4):
            size = hot.shape[0] // 4
            picks = one_hot_tiles(wide[here, :] - part * size, size // LANES)
            product = dot(picks, hot[part * size : (part + 1) * size, :])
            got = product if part == 0 else got + product
        extra[here, :] = got.astype(BF16)
        for part in range(256 // LANES):
            there = pl.ds(pl.multiple_of(first + part * LANES, LANES), LANES)

            def put(t, value):
                counts[t * LANES // chunk, there, t * LANES % chunk : t * LANES % chunk + LANES] = value

            count_tile(slots_sorted[:, there], fanout, tiles, lows, nibbles, put)
        return carry

    lax.fori_loop(0, slots // 256, build, 0)

    for t in range(edge // LANES):
        index = jnp.broadcast_to(halo_ref[:, t * LANES : (t + 1) * LANES], (8, LANES))
        picks = one_hot_tiles(turned(look_up(tables[1], index)[0:1, :]), tiles)
        last_counts[t * LANES : (t + 1) * LANES, 0:slots] = picks
        for c in range(chunks):
            edge_counts[c, edge + t * LANES : edge + (t + 1) * LANES, :] = picks[:, c * chunk : (c + 1) * chunk]

    def count_edge(c, carry):
        edge_counts[c, 0:edge, :] = dot(last_counts[0:edge, 0:slots], counts[c]).astype(BF16)
        return carry

    lax.fori_loop(0, chunks, count_edge, 0)

    def count_target(step, carry):
        there = pl.ds(pl.multiple_of(step * LANES, LANES), LANES)

        def put(t, value):
            last_counts[there, t * LANES : (t + 1) * LANES] = value

        count_tile(slots_next[:, there], fanout2, tiles + edge // LANES, lows, nibbles, put)
        own = pl.ds(pl.multiple_of(targets + step * LANES, LANES), LANES)
        last_counts[own, 0:slots] = one_hot_tiles(turned(rows[1:2, there]), tiles)
        return carry

    lax.fori_loop(0, targets // LANES, count_target, 0)

    total[...] = jnp.zeros_like(total)
    edge_total[...] = jnp.zeros_like(edge_total)

    def take(step):
        which = chunk_at(lax.rem(step + hosts, chunks), -1)

        def await_one(q, carry):
            peer = which * half + q

            @pl.when(peer != me)
            def _():
                away = lax.rem(me - peer + devices, devices)
                pltpu.make_async_remote_copy(
                    src_ref=outgoing.at[block(me)], dst_ref=arrived.at[block(peer)],
                    send_sem=send.at[away], recv_sem=recv.at[away], device_id=at(peer), device_id_type=MESH,
                ).wait_recv()

            return carry

        lax.fori_loop(0, half, await_one, 0)
        here = pl.ds(pl.multiple_of(which * chunk, chunk), chunk)
        mine = jnp.concatenate([wide[here, :]] * (width // LANES), axis=1) < 0
        chunk_rows[...] = jnp.where(mine, arrived[here, :].astype(F32), extra[here, :].astype(F32)).astype(BF16)
        edge_total[...] += dot(edge_counts[which], chunk_rows[...])

    def work(step):
        which = chunk_at(lax.rem(step + hosts, chunks), -1)
        here = pl.ds(pl.multiple_of(which * chunk, chunk), chunk)
        pre[here, :] = dot(chunk_rows[...], self_w[...])

        def gather(part, carry):
            there = pl.ds(pl.multiple_of(part * 512, 512), 512)
            total[there, :] += dot(counts[which, there, :], chunk_rows[...])
            return carry

        lax.fori_loop(0, slots // 512, gather, 0)

    def arrive(step, carry):
        take(step)
        work(step)
        return carry

    lax.fori_loop(0, chunks - 1, arrive, 0)
    take(chunks - 1)

    edge_mean = (edge_total[0:edge, :] * (1.0 / fanout)).astype(BF16)
    edge_pre = dot(edge_total[edge : 2 * edge, :].astype(BF16), self_w[...]) + dot(edge_mean, neigh_w[...])
    centre = jnp.mean(edge_pre, axis=0, keepdims=True)
    edge_out[...] = (edge_pre - centre).astype(BF16)

    def part_of(peer):
        return pl.ds(pl.multiple_of(peer * share, share), share)

    def edge_copy(peer):
        away = lax.rem(peer - lane + within, within)
        return pltpu.make_async_remote_copy(
            src_ref=edge_out.at[part_of(peer)], dst_ref=edge_in.at[part_of(lane)],
            send_sem=send_edge.at[away], recv_sem=recv_edge.at[away],
            device_id={"dev": peer}, device_id_type=MESH,
        )

    near_peers = [side * half + lax.rem(lane + q, half) for q in range(1, half)]
    far_peers = [lax.rem(side + 1, 2) * half + lax.rem(lane + q, half) for q in range(half)]
    for peer in far_peers[: half // 2] + near_peers:
        edge_copy(peer).start()
    edge_in[part_of(lane), :] = edge_out[part_of(lane), :]
    work(chunks - 1)

    shares = stat_own.shape[0]
    columns = units // shares
    near_copies, far_copies = {}, {}

    def swap(source, landing, axis, index, size, send_sem, recv_sem):
        copies = []
        for away in range(1, size):
            copies.append(pltpu.make_async_remote_copy(
                src_ref=source, dst_ref=landing.at[away - 1], send_sem=send_sem.at[away - 1],
                recv_sem=recv_sem.at[away - 1], device_id={axis: lax.rem(index + away, size)},
                device_id_type=MESH,
            ))
            copies[-1].start()
        return copies

    def gained(copies, source, landing):
        for copy in copies:
            copy.wait()
        value = source[...]
        for away in range(len(copies)):
            value = value + landing[away]
        return value

    def finish(q):
        there = slice(q * columns, (q + 1) * columns)

        def some(step, sums):
            here = pl.ds(pl.multiple_of(step * 512, 512), 512)
            if q == 0:
                extra[here, :] = (total[here, :] * (1.0 / fanout)).astype(BF16)
            value = pre[here, there] + dot(extra[here, :], neigh_w[:, there])
            pre[here, there] = value
            return (
                sums[0] + jnp.sum(value, axis=0, keepdims=True),
                sums[1] + jnp.sum(value * value, axis=0, keepdims=True),
            )

        zero = jnp.zeros((1, columns), F32)
        first, second = lax.fori_loop(0, slots // 512, some, (zero, zero))
        stat_own[q] = jnp.concatenate([first, second, centre[:, there], zero], axis=0)
        near_copies[q] = swap(
            stat_own.at[q], stat_near.at[q], "dev", lane, within, send_near.at[q], recv_near.at[q]
        )

    def relay(q):
        stat_part[q] = gained(near_copies[q], stat_own.at[q], stat_near.at[q])
        far_copies[q] = swap(stat_part.at[q], stat_far.at[q], "hst", host, hosts, send_far.at[q], recv_far.at[q])

    settled = {}

    def settle(q):
        there = slice(q * columns, (q + 1) * columns)
        sums = gained(far_copies[q], stat_part.at[q], stat_far.at[q])
        mean = sums[0:1, :] / total_rows
        variance = sums[1:2, :] / total_rows - mean * mean
        scale = lax.rsqrt(variance + epsilon) * gain_ref[:, there]
        shift = shift_ref[:, there]
        settled[q] = mean, scale, shift
        first_block = q * columns // chunk

        def normal(step, carry):
            here = pl.ds(pl.multiple_of(step * 256, 256), 256)
            hidden = jnp.maximum((pre[here, there] - mean) * scale + shift, 0.0).astype(BF16)
            for c in range(columns // chunk):
                counts[first_block + c, here, :] = hidden[:, c * chunk : (c + 1) * chunk]
            return carry

        lax.fori_loop(0, slots // 256, normal, 0)
        for c in range(columns // chunk):
            both = dot(last_counts[:, 0:slots], counts[first_block + c])
            total[q * targets : (q + 1) * targets, c * chunk : (c + 1) * chunk] = both[0:targets, :]
            at_column = q * columns + c * chunk
            value = dot_nt(self2_ref[:, at_column : at_column + chunk], both[targets:, :].astype(BF16))
            if at_column == 0:
                out_ref[...] = value
            else:
                out_ref[...] += value

    for q in range(shares):
        finish(q)
    for peer in far_peers[half // 2 :]:
        edge_copy(peer).start()
    for q in range(shares - 1):
        relay(q)
    settle(0)
    relay(shares - 1)
    for q in range(1, shares):
        settle(q)

    for away in range(1, within):
        edge_copy(lax.rem(lane + away, within)).wait()
    for q in range(shares):
        there = slice(q * columns, (q + 1) * columns)
        mean, scale, shift = settled[q]
        for away in range(within):
            place = part_of(lax.rem(lane - away + within, within))
            origin = centre[:, there] if away == 0 else stat_near[q, away - 1, 2:3, :]
            value = edge_in[place, there].astype(F32) + (origin - mean)
            edge_in[place, there] = jnp.maximum(value * scale + shift, 0.0).astype(BF16)
        near = total[q * targets : (q + 1) * targets, 0:columns]
        near = near + dot(last_counts[0:targets, slots:], edge_in[:, there])
        out_ref[...] += dot_nt(neigh2_ref[:, there], (near * (1.0 / fanout2)).astype(BF16))

    def drain(away, carry):
        row_copy(lax.rem(me + away, devices)).wait_send()
        return carry

    lax.fori_loop(1, devices, drain, 0)


def local(hot_rows, cold_rows, hot_mask, hot_id, cold_owner, cold_pos, cold_send, adjacency_one, adjacency_two,
          halo_send, self_first, neigh_first, bn_gain, bn_shift, self_second, neigh_second):
    hosts, within = lax.axis_size("hst"), lax.axis_size("dev")
    devices = hosts * within
    nodes, fanout = adjacency_one.shape
    targets, fanout2 = adjacency_two.shape
    slots, edge = cold_send.shape[1], halo_send.shape[1]
    width, units = self_first.shape
    classes = self_second.shape[1]
    assert slots == nodes
    chunk = slots // devices * (within // 2)
    chunks = slots // chunk
    lines = -(-(max(fanout, fanout2) + 1) // 8) * 8
    tiles = slots // LANES
    any_space, vmem = pl.BlockSpec(memory_space=pltpu.HBM), pl.BlockSpec(memory_space=pltpu.VMEM)
    dma = pltpu.SemaphoreType.DMA
    buffers = [pltpu.VMEM((1, nodes), I32) for _ in range(4)] + [
        pltpu.VMEM((1, slots), I32),
        pltpu.VMEM((fanout, nodes), I32),
        pltpu.VMEM((fanout2, targets), I32),
        pltpu.VMEM((1, edge), I32),
        pltpu.VMEM((1, units), F32),
        pltpu.VMEM((1, units), F32),
        pltpu.VMEM((classes, units), BF16),
        pltpu.VMEM((classes, units), BF16),
        pltpu.VMEM(cold_rows.shape, BF16),
        pltpu.VMEM((slots, width), BF16),
        pltpu.VMEM((slots, width), BF16),
        pltpu.VMEM(hot_rows.shape, BF16),
        pltpu.VMEM((slots, width), BF16),
        pltpu.VMEM((chunks, slots, chunk), BF16),
        pltpu.VMEM((chunks, 2 * edge, chunk), BF16),
        pltpu.VMEM((slots, width), F32),
        pltpu.VMEM((2 * edge, width), F32),
        pltpu.VMEM((slots, units), F32),
        pltpu.VMEM((2 * targets, slots + edge), BF16),
        pltpu.VMEM((width, units), BF16),
        pltpu.VMEM((width, units), BF16),
        pltpu.VMEM((edge, units), BF16),
        pltpu.VMEM((edge, units), BF16),
        pltpu.VMEM((slots, LANES), I32),
        pltpu.VMEM((lines, slots), I32),
        pltpu.VMEM((lines, slots), I32),
        pltpu.VMEM((lines, targets), I32),
        pltpu.VMEM((8, slots), I32),
        pltpu.VMEM((2, tiles, LANES), I32),
        pltpu.VMEM((lines, LANES), I32),
        pltpu.VMEM((-(-(tiles + edge // LANES) // 8), lines, LANES), I32),
        pltpu.VMEM((chunk, width), BF16),
        pltpu.VMEM((SHARES, 4, units // SHARES), F32),
        pltpu.VMEM((SHARES, within - 1, 4, units // SHARES), F32),
        pltpu.VMEM((SHARES, 4, units // SHARES), F32),
        pltpu.VMEM((SHARES, hosts - 1, 4, units // SHARES), F32),
    ]
    held = sum(math.prod(b.shape) * b.dtype.itemsize for b in buffers)
    out = pl.pallas_call(
        functools.partial(program, (hosts, within, fanout, fanout2, nodes * devices)),
        in_specs=[any_space] * 16,
        out_specs=vmem,
        out_shape=jax.ShapeDtypeStruct((classes, targets), F32),
        scratch_shapes=buffers + [
            dma((16,)),
            dma((devices,)),
            dma((devices,)),
            dma((within,)),
            dma((within,)),
            dma((SHARES, within - 1)),
            dma((SHARES, within - 1)),
            dma((SHARES, hosts - 1)),
            dma((SHARES, hosts - 1)),
        ],
        compiler_params=pltpu.CompilerParams(
            collective_id=0, has_side_effects=True, vmem_limit_bytes=min(held + 9 * MIB, 63 * MIB)
        ),
        name="sage",
    )(
        hot_rows, cold_rows, hot_mask[None, :], hot_id[None, :], cold_owner[None, :], cold_pos[None, :], cold_send,
        adjacency_one.T, adjacency_two.T, halo_send, self_first, neigh_first, bn_gain[None, :], bn_shift[None, :],
        self_second.T, neigh_second.T,
    )
    return out.T


def solution(mesh):
    owned, split, copied = P(("hst", "dev"), None), P(("hst", "dev")), P()
    placed = (copied, owned) + (split,) * 4 + (owned,) * 4 + (copied,) * 6
    return jax.shard_map(local, mesh=mesh, in_specs=placed, out_specs=owned, check_vma=False)
```

time: 124 us -> 109 us (0.88)
  Pallas kernels: 122 us -> 107 us
    pallas_call x1, Pallas kernels: 122 us -> 107 us  [local(): pl.pallas_call(functools.partial(program, (hosts, within, fanout, fanout2...]
where the time goes in v2:
time: 109 us
  Pallas kernels  107 us (98%)
  local copies, waits for them, and re-layouts  1.72 us (2%)
    pallas_call x1, Pallas kernels, local(): pl.pallas_call(functools.partial(program, (hosts, within, fanout, fanout2...  107 us

profile of v2, /device:TPU:0, one launch (start us, length us, event | category | flops | bytes accessed | tf_op | source)
XLA Modules:
  0.0 108.5 jit_solution(2821788346382938649)
XLA Ops:
  0.0 106.8 %sage.1 = f32[153,512]{1,0:T(8,128)} custom-call(bf16[4096,768]{1,0:T(8,128)(2,1)} %hot_hbm.1, bf16[1024,768]{1,0:T(8,128)(2,1)} %cold_hbm.1, s32[1,2048]{1,0:T(1,128)} %bitcast.16, s32[1,2048]{1,0:T(1,128)} %bitcast.17, s32[1,2048]{1,0:T(1,128)} %bitcast.18, s32[1,2048]{1,0:T(1,128)} %bitcast.19, s32[1,2048]{1,0:T(1,128)} %send_hbm.1, s32[15,2048]{1,0:T(8,128)} %bitcast.14, ...), custom_call_target="tpu_custom_call" | custom-call | tf_op jit(solution)/shard_map/sage/pallas_call | solution.py:540
  106.8 1.7 %copy.18 = f32[512,153]{0,1:T(8,128)} copy(f32[512,153]{0,1:T(8,128)} %bitcast.11) | data formatting | bytes 626688
